TPU v7x, 128 devices: a whole 4x4x4 slice. The times are simulated.
128 devices in a mesh: lat: 4 (over z), lon: 32 (over x, y, core).
Axes of the slice: x: 4, y: 4, z: 4, core: 2. Of those that a mesh axis runs over, the one named last changes fastest.
Arguments:
- spectrum: float32 [1296, 32, 8192], P(None, 'lat', 'lon'), may hold values from 0.01 to 1
- sea_mask: int32 [32, 8192], P('lat', 'lon'), may hold values 0 or 1
- courant: float32 [2, 1296], replicated, may hold values from -0.45 to 0.45
- obs_tile: int32 [32768, 1], P(('lat', 'lon')), may hold values from 0 to 127; in each aligned block of 256 rows (0 to 255, 256 to 511, ...) at most 8 rows name the same one
- obs_cell: int32 [32768], P(('lat', 'lon')), may hold values from 0 to 2047
- obs_value: float32 [32768], P(('lat', 'lon')), may hold values from 1 to 3
- obs_error: float32 [32768], P(('lat', 'lon')), may hold values from 0.05 to 0.5
Outputs:
- updated: float32 [1296, 32, 8192], P(None, 'lat', 'lon')
- increment: float32 [32, 8192], P('lat', 'lon')
Inputs may be any that keep to these rules, and one draw needn't show every extreme that they name: `obs_tile`: within the 256 reports of one device no tile occurs more than 8 times.
All inputs are finite; a program needn't handle non-finite values. No bound on the sum of `sea_mask` on one device may be relied on, other than what follows from the above.
Results may differ from a plain program's by a relative error of at most 0.00002.
Values sent between devices are 32-bit elements; how exact they have to be, the bound alone decides.
A program may use at most 128 MiB of HBM per device.

v0:
```python
import jax
import jax.numpy as jnp
from jax import lax
from jax.sharding import PartitionSpec as P

PASSES = 8
spread_rate = 0.2
prior_weight = 4.0


def with_halo(array, sides, width):
    edges = {}
    for axis, dim in sides:
        size, length = (lax.axis_size(axis), array.shape[dim])
        up = [(i, (i + 1) % size) for i in range(size)]
        last = lax.slice_in_dim(array, length - width, length, axis=dim)
        leading = lax.slice_in_dim(array, 0, width, axis=dim)
        edges[dim] = (
            lax.ppermute(last, axis, up),
            lax.ppermute(leading, axis, [(b, a) for a, b in up]),
        )
    done = []
    for _, dim in sides:
        low, high = edges[dim]
        around = [(width, width) if d in done else (0, 0) for d in range(array.ndim)]
        array = jnp.concatenate([jnp.pad(low, around), array, jnp.pad(high, around)], axis=dim)
        done.append(dim)
    return array


def with_halo_2(cells, sides, width):
    for axis, dim in sides:
        count = lax.axis_size(axis)
        head = lax.slice_in_dim(cells, 0, width, axis=dim)
        tail = lax.slice_in_dim(cells, cells.shape[dim] - width, cells.shape[dim], axis=dim)
        cells = jnp.concatenate(
            [
                lax.ppermute(tail, axis, [(i, (i + 1) % count) for i in range(count)]),
                cells,
                lax.ppermute(head, axis, [((i + 1) % count, i) for i in range(count)]),
            ],
            axis=dim,
        )
    return cells


def relax_pass(fields, sea_ext):
    centre = fields[:, 1:-1, 1:-1]
    summed = sea_ext[2:, 1:-1] * (fields[:, 2:, 1:-1] - centre)
    summed = summed + sea_ext[:-2, 1:-1] * (fields[:, :-2, 1:-1] - centre)
    summed = summed + sea_ext[1:-1, 2:] * (fields[:, 1:-1, 2:] - centre)
    summed = summed + sea_ext[1:-1, :-2] * (fields[:, 1:-1, :-2] - centre)
    return centre + spread_rate * sea_ext[1:-1, 1:-1] * summed


def body(spectrum, sea_mask, courant, obs_tile, obs_cell, obs_value, obs_error):
    tile_rows, tile_cols = sea_mask.shape
    lat_count = lax.axis_size("lat")
    lon_count = lax.axis_size("lon")
    devices = lat_count * lon_count
    report_count = obs_value.shape[0]
    slot_cap = max(8, 4 * report_count // devices)
    outer_rim = with_halo(spectrum, (("lat", 1), ("lon", 2)), 1)
    height = 4.0 * jnp.sqrt(jnp.mean(spectrum, axis=0))
    height_flat = height.reshape(-1)
    weights = 1.0 / obs_error
    owners = obs_tile[:, 0]
    blank_grid = jnp.zeros((2, tile_rows * tile_cols), jnp.float32)
    position = jnp.arange(report_count, dtype=jnp.int32)
    earlier = (owners[:, None] == owners[None, :]) & (position[None, :] < position[:, None])
    slot_index = jnp.sum(earlier.astype(jnp.int32), axis=1)
    reports = jnp.stack([obs_value, weights, obs_cell.astype(jnp.float32)])
    outbox = (
        jnp.zeros((3, devices, slot_cap), jnp.float32)
        .at[:, owners, slot_index]
        .set(reports)
        .reshape(3, lat_count, lon_count, slot_cap)
    )
    arrived = lax.all_to_all(
        lax.all_to_all(outbox, "lat", split_axis=1, concat_axis=1, tiled=True),
        "lon",
        split_axis=2,
        concat_axis=2,
        tiled=True,
    ).reshape(3, -1)
    totals = blank_grid
    cell_ids = arrived[2].astype(jnp.int32)
    report_weights = arrived[1]
    misfit = report_weights * (arrived[0] - height_flat[cell_ids])
    totals = totals.at[0, cell_ids].add(misfit)
    totals = totals.at[1, cell_ids].add(report_weights)
    ocean = sea_mask.astype(jnp.float32)
    fields = totals.reshape(2, tile_rows, tile_cols) * ocean
    halo_depth = 2
    coast_ext = with_halo_2(sea_mask, (("lat", 0), ("lon", 1)), halo_depth)
    lat_line = (
        lax.axis_index("lat") * tile_rows
        + jnp.arange(tile_rows + 2 * halo_depth, dtype=jnp.int32)
        - halo_depth
    )
    inside = (lat_line >= 0) & (lat_line < lat_count * tile_rows)
    coast_ext = jnp.where(inside[:, None], coast_ext, 0).astype(jnp.float32)
    edge_sea = coast_ext[
        halo_depth - 1 : coast_ext.shape[0] - halo_depth + 1,
        halo_depth - 1 : coast_ext.shape[1] - halo_depth + 1,
    ]
    for repeat in range(PASSES // 2):
        padded = with_halo_2(fields, (("lat", 1), ("lon", 2)), 2)
        fields = relax_pass(relax_pass(padded, coast_ext), edge_sea)
    increment = ocean * fields[0] / (prior_weight + fields[1])
    factor = jnp.exp(2.0 * increment / height)
    rim_scale = with_halo_2(factor, (("lat", 0), ("lon", 1)), 1)
    analyzed = outer_rim * rim_scale
    east_speed = courant[0][:, None, None]
    north_speed = courant[1][:, None, None]
    row_band = analyzed[:, 1:-1, :]
    ocean_band = edge_sea[1:-1, :]
    flux_east = (
        (
            jnp.maximum(east_speed, 0.0) * row_band[:, :, :-1]
            + jnp.minimum(east_speed, 0.0) * row_band[:, :, 1:]
        )
        * ocean_band[:, :-1]
        * ocean_band[:, 1:]
    )
    col_strip = analyzed[:, :, 1:-1]
    ocean_strip = edge_sea[:, 1:-1]
    flux_north = (
        (
            jnp.maximum(north_speed, 0.0) * col_strip[:, :-1]
            + jnp.minimum(north_speed, 0.0) * col_strip[:, 1:]
        )
        * ocean_strip[:-1]
        * ocean_strip[1:]
    )
    centre = analyzed[:, 1:-1, 1:-1]
    updated = ocean * (
        centre
        - (flux_east[:, :, 1:] - flux_east[:, :, :-1])
        - (flux_north[:, 1:] - flux_north[:, :-1])
    )
    return (updated, increment)


def solution(mesh):
    return jax.shard_map(
        body,
        mesh=mesh,
        in_specs=(
            P(None, "lat", "lon"),
            P("lat", "lon"),
            P(),
            P(("lat", "lon"), None),
            P(("lat", "lon")),
            P(("lat", "lon")),
            P(("lat", "lon")),
        ),
        out_specs=(P(None, "lat", "lon"), P("lat", "lon")),
        check_vma=False,
    )
```

profile of v0, /device:TPU:1, one launch (start us, length us, event | category | flops | bytes accessed | tf_op | source)
XLA Modules:
  0.0 246.1 jit_solution(15258800450788764085)
XLA Ops:
  9.9 11.5 %scatter_fusion = f32[3,128,8]{0,2,1:T(8,128)S(1)} fusion(f32[3,128,8]{0,2,1:T(8,128)S(1)} %broadcast_in_dim.13, s32[256]{0:T(256)S(1)} %bitcast.35, f32[256,3]{1,0:T(8,128)S(1)} %copy.52), kind=kCustom, calls=%fused_computation.1 | custom fusion | bytes 11264 | tf_op jit(solution)/shard_map/scatter | solution.py:76
  22.4 3.3 %all-to-all-start = ((f32[4,1,768]{2,1,0:T(1,128)}), f32[4,1,768]{2,1,0:T(1,128)S(1)}, u32[]{:S(2)}, u32[]{:S(2)}) async-start(f32[4,1,768]{2,1,0:T(1,128)} %reshape.164), calls=%async_computation | async-start | bytes 24576 | tf_op jit(solution)/shard_map/all_to_all | solution.py:80
  25.6 4.8 %reduce_sum.22 = f32[8,256]{1,0:T(8,128)S(1)} reduce(f32[1296,8,256]{2,1,0:T(8,128)} %param.7, f32[]{:T(128)} %constant.15.clone.1), dimensions={0}, to_apply=%region_2.3 | reduce | flops 2652160 | bytes 10625028 | tf_op jit(solution)/shard_map/reduce_sum | solution.py:64
  34.9 7.7 %all-to-all-start.1 = ((f32[3,4,32,8]{3,1,0,2:T(4,128)}), f32[3,4,32,8]{3,1,0,2:T(4,128)S(1)}, u32[]{:S(2)}, u32[]{:S(2)}) async-start(f32[3,4,32,8]{3,1,0,2:T(4,128)} %copy.54), calls=%async_computation.1 | async-start | bytes 393216 | tf_op jit(solution)/shard_map/all_to_all | solution.py:79
  42.6 8.2 %all-to-all-done.1 = f32[3,4,32,8]{3,1,0,2:T(4,128)S(1)} async-done(((f32[3,4,32,8]{3,1,0,2:T(4,128)}), f32[3,4,32,8]{3,1,0,2:T(4,128)S(1)}, u32[]{:S(2)}, u32[]{:S(2)}) %all-to-all-start.1) | async-done | bytes 12320 | tf_op jit(solution)/shard_map/all_to_all | solution.py:79
  51.6 6.2 %gather_fusion = f32[1024]{0:T(1024)S(1)} fusion(f32[2048]{0:T(1024)S(1)} %bitcast.34, s32[1024]{0:T(1024)S(1)} %broadcast_clamp_fusion), kind=kCustom, calls=%fused_computation | custom fusion | bytes 12288 | tf_op jit(solution)/shard_map/gather | solution.py:89
  57.8 7.0 %scatter_custom_fusion.1 = f32[4096]{0:T(1024)S(1)} fusion(s32[1024]{0:T(1024)S(1)} %get-tuple-element.64, f32[1024]{0:T(1024)S(1)} %subtract_multiply_fusion, f32[]{:T(128)} %constant.15.clone.1), kind=kCustom, calls=%fused_computation.182 | custom fusion | flops 1024 | bytes 16388
  64.8 7.1 %scatter_fusion.1 = f32[4096]{0:T(1024)S(1)} fusion(f32[4096]{0:T(1024)S(1)} %scatter_custom_fusion.1, s32[1024]{0:T(1024)S(1)} %get-tuple-element.63, f32[1024]{0:T(1024)S(1)} %reshape.154), kind=kCustom, calls=%fused_computation.3 | custom fusion | flops 1024 | bytes 16384
  83.0 9.2 %fusion.102 = (f32[1296,1,256]{2,1,0:T(1,128)S(1)}, f32[1296,1,256]{2,1,0:T(1,128)S(1)}) fusion(f32[1296,8,256]{2,1,0:T(8,128)} %param.7), kind=kLoop, calls=%fused_computation.205 | loop fusion | bytes 5308416 | tf_op jit(solution)/shard_map/slice | solution.py:16
  93.4 5.8 %collective-permute-start.15 = (f32[2,12,2]{2,1,0:T(8,128)S(1)}, f32[2,12,2]{2,1,0:T(8,128)S(1)}, u32[]{:S(2)}, u32[]{:S(2)}) collective-permute-start(f32[2,12,2]{2,1,0:T(8,128)S(1)} %get-tuple-element.29), channel_id=1, source_target_pairs={{1,0},{2,1},{3,2},{4,3},{5,4},{6,5},{7,6},{8,7},{9,8},{10,9},{11,1... | collective-permute-start | bytes 584 | tf_op jit(solution)/shard_map/ppermute | solution.py:40
  103.5 7.5 %fusion.103 = (f32[1296,8,1]{2,1,0:T(8,128)}, f32[1296,8,1]{2,1,0:T(8,128)}) fusion(f32[1296,8,256]{2,1,0:T(8,128)} %param.7), kind=kLoop, calls=%fused_computation.206 | loop fusion | bytes 165888 | tf_op jit(solution)/shard_map/slice | solution.py:16
  111.0 20.1 %collective-permute-done.16 = f32[2,2,256]{2,1,0:T(2,128)S(1)} collective-permute-done((f32[2,2,256]{2,1,0:T(2,128)S(1)}, f32[2,2,256]{2,1,0:T(2,128)S(1)}, u32[]{:S(2)}, u32[]{:S(2)}) %collective-permute-start.16) | collective-permute-done | bytes 4128 | tf_op jit(solution)/shard_map/ppermute | solution.py:38
  133.0 4.1 %copy.63 = f32[1296,8,1]{0,1,2:T(8,128)S(1)} copy(f32[1296,8,1]{2,1,0:T(8,128)} %get-tuple-element.21) | data formatting | bytes 82944
  140.5 12.4 %copy.47 = f32[1296,8,256]{0,2,1:T(8,128)} copy(f32[1296,8,256]{2,1,0:T(8,128)} %param.7) | data formatting | bytes 21233664 | tf_op args[0]
  152.9 4.1 %copy.60 = f32[1296,8,1]{0,1,2:T(8,128)S(1)} copy(f32[1296,8,1]{2,1,0:T(8,128)} %get-tuple-element.20) | data formatting | bytes 82944
  157.1 5.2 %collective-permute-start.23 = (f32[2,12,2]{2,1,0:T(8,128)S(1)}, f32[2,12,2]{2,1,0:T(8,128)S(1)}, u32[]{:S(2)}, u32[]{:S(2)}) collective-permute-start(f32[2,12,2]{2,1,0:T(8,128)S(1)} %get-tuple-element.25), channel_id=1, source_target_pairs={{1,0},{2,1},{3,2},{4,3},{5,4},{6,5},{7,6},{8,7},{9,8},{10,9},{11,1... | collective-permute-start | bytes 584 | tf_op jit(solution)/shard_map/ppermute | solution.py:40
  168.4 2.8 %collective-permute-start = (f32[1296,8,1]{0,1,2:T(8,128)S(1)}, f32[1296,8,1]{0,1,2:T(8,128)S(1)}, u32[]{:S(2)}, u32[]{:S(2)}) collective-permute-start(f32[1296,8,1]{0,1,2:T(8,128)S(1)} %copy.60), channel_id=1, source_target_pairs={{0,1},{1,2},{2,3},{3,4},{4,5},{5,6},{6,7},{7,8},{8,9},{9,10},{10,1... | collective-permute-start | bytes 124424 | tf_op jit(solution)/shard_map/ppermute | solution.py:19
  171.3 4.1 %collective-permute-done.26 = f32[10,1]{1,0:T(8,128)S(1)} collective-permute-done((f32[10,1]{1,0:T(8,128)S(1)}, f32[10,1]{1,0:T(8,128)S(1)}, u32[]{:S(2)}, u32[]{:S(2)}) %collective-permute-start.26) | collective-permute-done | bytes 72 | tf_op jit(solution)/shard_map/ppermute | solution.py:38
  175.4 6.1 %collective-permute-start.27 = (f32[10,1]{1,0:T(8,128)S(1)}, f32[10,1]{1,0:T(8,128)S(1)}, u32[]{:S(2)}, u32[]{:S(2)}) collective-permute-start(f32[10,1]{1,0:T(8,128)S(1)} %get-tuple-element.48), channel_id=1, source_target_pairs={{1,0},{2,1},{3,2},{4,3},{5,4},{6,5},{7,6},{8,7},{9,8},{10,9},{11,1... | collective-permute-start | bytes 128 | tf_op jit(solution)/shard_map/ppermute | solution.py:40
  186.1 14.5 %fusion = f32[1296,10,258]{0,2,1:T(8,128)S(1)} fusion(f32[1296,8,1]{0,2,1:T(1,128)S(1)} %copy.66, f32[1296,8,1]{0,2,1:T(1,128)S(1)} %copy.65, f32[1296,1,256]{0,2,1:T(8,128)S(1)} %copy.48, f32[1296,8,256]{0,2,1:T(8,128)} %copy.47, f32[1296,1,256]{0,2,1:T(8,128)S(1)} %copy.46, f32[10,258]{1,0:T(8,128)S(1)} %pad_maximum_fusion.32), kind=kLoop, calls=%fused_computation.5 | loop fusion | flops 30093120 | bytes 26739024 | tf_op jit(solution)/shard_map/mul | solution.py:113
  200.5 5.9 %fusion.6 = f32[1296,8,257]{0,2,1:T(8,128)} fusion(f32[1296,10,258]{0,2,1:T(8,128)S(1)} %fusion, f32[8,257]{1,0:T(8,128)S(1)} %get-tuple-element.34, f32[8,257]{1,0:T(8,128)S(1)} %get-tuple-element.33, f32[1296]{0:T(1024)S(1)} %get-tuple-element.9, f32[1296]{0:T(1024)S(1)} %get-tuple-element.8), kind=kLoop, calls=%fused_computation.17 | loop fusion | flops 13322880 | bytes 32001728 | tf_op jit(solution)/shard_map/mul | solution.py:119
  206.4 7.3 %fusion.3 = f32[1296,9,256]{0,2,1:T(8,128)} fusion(f32[1296,10,258]{0,2,1:T(8,128)S(1)} %fusion, f32[9,256]{1,0:T(8,128)S(1)} %get-tuple-element.36, f32[9,256]{1,0:T(8,128)S(1)} %get-tuple-element.35, f32[1296]{0:T(1024)S(1)} %get-tuple-element.10, f32[1296]{0:T(1024)S(1)} %get-tuple-element.11), kind=kLoop, calls=%fused_computation.12 | loop fusion | flops 14929920 | bytes 35860608 | tf_op jit(solution)/shard_map/mul | solution.py:129
  213.8 20.2 %fusion.8 = f32[1296,8,256]{0,2,1:T(8,128)} fusion(f32[1296,9,256]{0,2,1:T(8,128)} %fusion.3, f32[1296,8,257]{0,2,1:T(8,128)} %fusion.6, f32[1296,10,258]{0,2,1:T(8,128)S(1)} %fusion, f32[8,256]{1,0:T(8,128)S(1)} %convert_element_type.28), kind=kLoop, calls=%fused_computation.21 | loop fusion | flops 13271040 | bytes 63709184 | tf_op jit(solution)/shard_map/mul | solution.py:137
  234.0 12.1 %copy.59 = f32[1296,8,256]{2,1,0:T(8,128)} copy(f32[1296,8,256]{0,2,1:T(8,128)} %fusion.8) | data formatting | bytes 21233664
  (137 shorter events, 47.8 us)
Async XLA Ops:
  1.5 29.0 %collective-permute-start.8 = (s32[2,256]{1,0:T(2,128)S(1)}, s32[2,256]{1,0:T(2,128)S(1)}, u32[]{:S(2)}, u32[]{:S(2)}) collective-permute-start(s32[2,256]{1,0:T(2,128)S(1)} %get-tuple-element.61), channel_id=1, source_target_pairs={{0,32},{32,64},{64,96},{96,0},{1,33},{33,65},{65,97},{97,1},{2,34}... | collective-permute-start | bytes 6152 | tf_op jit(solution)/shard_map/ppermute | solution.py:38
  3.9 26.6 %collective-permute-start.9 = (s32[2,256]{1,0:T(2,128)S(1)}, s32[2,256]{1,0:T(2,128)S(1)}, u32[]{:S(2)}, u32[]{:S(2)}) collective-permute-start(s32[2,256]{1,0:T(2,128)S(1)} %get-tuple-element.62), channel_id=1, source_target_pairs={{32,0},{64,32},{96,64},{0,96},{33,1},{65,33},{97,65},{1,97},{34,2}... | collective-permute-start | bytes 6152 | tf_op jit(solution)/shard_map/ppermute | solution.py:40
  22.4 10.4 %all-to-all-start = ((f32[4,1,768]{2,1,0:T(1,128)}), f32[4,1,768]{2,1,0:T(1,128)S(1)}, u32[]{:S(2)}, u32[]{:S(2)}) async-start(f32[4,1,768]{2,1,0:T(1,128)} %reshape.164), calls=%async_computation | async-start | bytes 24576 | tf_op jit(solution)/shard_map/all_to_all | solution.py:80
  30.6 11.9 %collective-permute-start.10 = (s32[12,2]{1,0:T(8,128)S(1)}, s32[12,2]{1,0:T(8,128)S(1)}, u32[]{:S(2)}, u32[]{:S(2)}) collective-permute-start(s32[12,2]{1,0:T(8,128)S(1)} %get-tuple-element.55), channel_id=1, source_target_pairs={{0,1},{1,2},{2,3},{3,4},{4,5},{5,6},{6,7},{7,8},{8,9},{9,10},{10,1... | collective-permute-start | bytes 296 | tf_op jit(solution)/shard_map/ppermute | solution.py:38
  32.8 9.8 %collective-permute-start.11 = (s32[12,2]{1,0:T(8,128)S(1)}, s32[12,2]{1,0:T(8,128)S(1)}, u32[]{:S(2)}, u32[]{:S(2)}) collective-permute-start(s32[12,2]{1,0:T(8,128)S(1)} %get-tuple-element.56), channel_id=1, source_target_pairs={{1,0},{2,1},{3,2},{4,3},{5,4},{6,5},{7,6},{8,7},{9,8},{10,9},{11,1... | collective-permute-start | bytes 296 | tf_op jit(solution)/shard_map/ppermute | solution.py:40
  34.9 16.0 %all-to-all-start.1 = ((f32[3,4,32,8]{3,1,0,2:T(4,128)}), f32[3,4,32,8]{3,1,0,2:T(4,128)S(1)}, u32[]{:S(2)}, u32[]{:S(2)}) async-start(f32[3,4,32,8]{3,1,0,2:T(4,128)} %copy.54), calls=%async_computation.1 | async-start | bytes 393216 | tf_op jit(solution)/shard_map/all_to_all | solution.py:79
  80.3 13.1 %collective-permute-start.12 = (f32[2,2,256]{2,1,0:T(2,128)S(1)}, f32[2,2,256]{2,1,0:T(2,128)S(1)}, u32[]{:S(2)}, u32[]{:S(2)}) collective-permute-start(f32[2,2,256]{2,1,0:T(2,128)S(1)} %get-tuple-element.53), channel_id=1, source_target_pairs={{0,32},{32,64},{64,96},{96,0},{1,33},{33,65},{65,97},{97,1},{2,34}... | collective-permute-start | bytes 12296 | tf_op jit(solution)/shard_map/ppermute | solution.py:38
  81.1 12.2 %collective-permute-start.13 = (f32[2,2,256]{2,1,0:T(2,128)S(1)}, f32[2,2,256]{2,1,0:T(2,128)S(1)}, u32[]{:S(2)}, u32[]{:S(2)}) collective-permute-start(f32[2,2,256]{2,1,0:T(2,128)S(1)} %get-tuple-element.54), channel_id=1, source_target_pairs={{32,0},{64,32},{96,64},{0,96},{33,1},{65,33},{97,65},{1,97},{34,2}... | collective-permute-start | bytes 12296 | tf_op jit(solution)/shard_map/ppermute | solution.py:40
  92.3 90.2 %collective-permute-start.2 = (f32[1296,1,256]{2,0,1:T(8,128)S(1)}, f32[1296,1,256]{2,0,1:T(8,128)}, u32[]{:S(2)}, u32[]{:S(2)}) collective-permute-start(f32[1296,1,256]{2,0,1:T(8,128)S(1)} %copy.62), channel_id=1, source_target_pairs={{32,0},{64,32},{96,64},{0,96},{33,1},{65,33},{97,65},{1,97},{34,2}... | collective-permute-start | bytes 3981320 | tf_op jit(solution)/shard_map/ppermute | solution.py:20
  93.4 6.7 %collective-permute-start.15 = (f32[2,12,2]{2,1,0:T(8,128)S(1)}, f32[2,12,2]{2,1,0:T(8,128)S(1)}, u32[]{:S(2)}, u32[]{:S(2)}) collective-permute-start(f32[2,12,2]{2,1,0:T(8,128)S(1)} %get-tuple-element.29), channel_id=1, source_target_pairs={{1,0},{2,1},{3,2},{4,3},{5,4},{6,5},{7,6},{8,7},{9,8},{10,9},{11,1... | collective-permute-start | bytes 584 | tf_op jit(solution)/shard_map/ppermute | solution.py:40
  99.3 85.0 %collective-permute-start.1 = (f32[1296,1,256]{2,0,1:T(8,128)S(1)}, f32[1296,1,256]{2,0,1:T(8,128)}, u32[]{:S(2)}, u32[]{:S(2)}) collective-permute-start(f32[1296,1,256]{2,0,1:T(8,128)S(1)} %copy.61), channel_id=1, source_target_pairs={{0,32},{32,64},{64,96},{96,0},{1,33},{33,65},{65,97},{97,1},{2,34}... | collective-permute-start | bytes 3981320 | tf_op jit(solution)/shard_map/ppermute | solution.py:19
  100.8 30.4 %collective-permute-start.16 = (f32[2,2,256]{2,1,0:T(2,128)S(1)}, f32[2,2,256]{2,1,0:T(2,128)S(1)}, u32[]{:S(2)}, u32[]{:S(2)}) collective-permute-start(f32[2,2,256]{2,1,0:T(2,128)S(1)} %get-tuple-element.51), channel_id=1, source_target_pairs={{0,32},{32,64},{64,96},{96,0},{1,33},{33,65},{65,97},{97,1},{2,34}... | collective-permute-start | bytes 12296 | tf_op jit(solution)/shard_map/ppermute | solution.py:38
  101.2 29.9 %collective-permute-start.17 = (f32[2,2,256]{2,1,0:T(2,128)S(1)}, f32[2,2,256]{2,1,0:T(2,128)S(1)}, u32[]{:S(2)}, u32[]{:S(2)}) collective-permute-start(f32[2,2,256]{2,1,0:T(2,128)S(1)} %get-tuple-element.52), channel_id=1, source_target_pairs={{32,0},{64,32},{96,64},{0,96},{33,1},{65,33},{97,65},{1,97},{34,2}... | collective-permute-start | bytes 12296 | tf_op jit(solution)/shard_map/ppermute | solution.py:40
  131.3 6.0 %collective-permute-start.19 = (f32[2,12,2]{2,1,0:T(8,128)S(1)}, f32[2,12,2]{2,1,0:T(8,128)S(1)}, u32[]{:S(2)}, u32[]{:S(2)}) collective-permute-start(f32[2,12,2]{2,1,0:T(8,128)S(1)} %get-tuple-element.27), channel_id=1, source_target_pairs={{1,0},{2,1},{3,2},{4,3},{5,4},{6,5},{7,6},{8,7},{9,8},{10,9},{11,1... | collective-permute-start | bytes 584 | tf_op jit(solution)/shard_map/ppermute | solution.py:40
  132.6 4.7 %collective-permute-start.18 = (f32[2,12,2]{2,1,0:T(8,128)S(1)}, f32[2,12,2]{2,1,0:T(8,128)S(1)}, u32[]{:S(2)}, u32[]{:S(2)}) collective-permute-start(f32[2,12,2]{2,1,0:T(8,128)S(1)} %get-tuple-element.28), channel_id=1, source_target_pairs={{0,1},{1,2},{2,3},{3,4},{4,5},{5,6},{6,7},{7,8},{8,9},{9,10},{10,1... | collective-permute-start | bytes 584 | tf_op jit(solution)/shard_map/ppermute | solution.py:38
  137.1 45.3 %collective-permute-start.3 = (f32[1296,8,1]{0,1,2:T(8,128)S(1)}, f32[1296,8,1]{0,1,2:T(8,128)S(1)}, u32[]{:S(2)}, u32[]{:S(2)}) collective-permute-start(f32[1296,8,1]{0,1,2:T(8,128)S(1)} %copy.63), channel_id=1, source_target_pairs={{1,0},{2,1},{3,2},{4,3},{5,4},{6,5},{7,6},{8,7},{9,8},{10,9},{11,1... | collective-permute-start | bytes 124424 | tf_op jit(solution)/shard_map/ppermute | solution.py:20
  137.6 19.3 %collective-permute-start.20 = (f32[2,2,256]{2,1,0:T(2,128)S(1)}, f32[2,2,256]{2,1,0:T(2,128)S(1)}, u32[]{:S(2)}, u32[]{:S(2)}) collective-permute-start(f32[2,2,256]{2,1,0:T(2,128)S(1)} %get-tuple-element.49), channel_id=1, source_target_pairs={{0,32},{32,64},{64,96},{96,0},{1,33},{33,65},{65,97},{97,1},{2,34}... | collective-permute-start | bytes 12296 | tf_op jit(solution)/shard_map/ppermute | solution.py:38
  137.7 19.3 %collective-permute-start.21 = (f32[2,2,256]{2,1,0:T(2,128)S(1)}, f32[2,2,256]{2,1,0:T(2,128)S(1)}, u32[]{:S(2)}, u32[]{:S(2)}) collective-permute-start(f32[2,2,256]{2,1,0:T(2,128)S(1)} %get-tuple-element.50), channel_id=1, source_target_pairs={{32,0},{64,32},{96,64},{0,96},{33,1},{65,33},{97,65},{1,97},{34,2}... | collective-permute-start | bytes 12296 | tf_op jit(solution)/shard_map/ppermute | solution.py:40
  157.1 6.0 %collective-permute-start.23 = (f32[2,12,2]{2,1,0:T(8,128)S(1)}, f32[2,12,2]{2,1,0:T(8,128)S(1)}, u32[]{:S(2)}, u32[]{:S(2)}) collective-permute-start(f32[2,12,2]{2,1,0:T(8,128)S(1)} %get-tuple-element.25), channel_id=1, source_target_pairs={{1,0},{2,1},{3,2},{4,3},{5,4},{6,5},{7,6},{8,7},{9,8},{10,9},{11,1... | collective-permute-start | bytes 584 | tf_op jit(solution)/shard_map/ppermute | solution.py:40
  164.4 3.9 %collective-permute-start.24 = (f32[1,256]{1,0:T(1,128)S(1)}, f32[1,256]{1,0:T(1,128)S(1)}, u32[]{:S(2)}, u32[]{:S(2)}) collective-permute-start(f32[1,256]{1,0:T(1,128)S(1)} %get-tuple-element.59), channel_id=1, source_target_pairs={{0,32},{32,64},{64,96},{96,0},{1,33},{33,65},{65,97},{97,1},{2,34}... | collective-permute-start | bytes 3080 | tf_op jit(solution)/shard_map/ppermute | solution.py:38
  164.4 6.8 %collective-permute-start.25 = (f32[1,256]{1,0:T(1,128)S(1)}, f32[1,256]{1,0:T(1,128)S(1)}, u32[]{:S(2)}, u32[]{:S(2)}) collective-permute-start(f32[1,256]{1,0:T(1,128)S(1)} %get-tuple-element.60), channel_id=1, source_target_pairs={{32,0},{64,32},{96,64},{0,96},{33,1},{65,33},{97,65},{1,97},{34,2}... | collective-permute-start | bytes 3080 | tf_op jit(solution)/shard_map/ppermute | solution.py:40
  168.4 14.1 %collective-permute-start = (f32[1296,8,1]{0,1,2:T(8,128)S(1)}, f32[1296,8,1]{0,1,2:T(8,128)S(1)}, u32[]{:S(2)}, u32[]{:S(2)}) collective-permute-start(f32[1296,8,1]{0,1,2:T(8,128)S(1)} %copy.60), channel_id=1, source_target_pairs={{0,1},{1,2},{2,3},{3,4},{4,5},{5,6},{6,7},{7,8},{8,9},{9,10},{10,1... | collective-permute-start | bytes 124424 | tf_op jit(solution)/shard_map/ppermute | solution.py:19
  171.3 4.1 %collective-permute-start.26 = (f32[10,1]{1,0:T(8,128)S(1)}, f32[10,1]{1,0:T(8,128)S(1)}, u32[]{:S(2)}, u32[]{:S(2)}) collective-permute-start(f32[10,1]{1,0:T(8,128)S(1)} %get-tuple-element.47), channel_id=1, source_target_pairs={{0,1},{1,2},{2,3},{3,4},{4,5},{5,6},{6,7},{7,8},{8,9},{9,10},{10,1... | collective-permute-start | bytes 128 | tf_op jit(solution)/shard_map/ppermute | solution.py:38
  175.4 6.9 %collective-permute-start.27 = (f32[10,1]{1,0:T(8,128)S(1)}, f32[10,1]{1,0:T(8,128)S(1)}, u32[]{:S(2)}, u32[]{:S(2)}) collective-permute-start(f32[10,1]{1,0:T(8,128)S(1)} %get-tuple-element.48), channel_id=1, source_target_pairs={{1,0},{2,1},{3,2},{4,3},{5,4},{6,5},{7,6},{8,7},{9,8},{10,9},{11,1... | collective-permute-start | bytes 128 | tf_op jit(solution)/shard_map/ppermute | solution.py:40
  (10 other events, 184.0 us)
where the time goes:
time: 247 us; the launch traced here: 246 us
  local copies, waits for them, and re-layouts  75.3 us (30%)
  other arithmetic  73.7 us (30%)
  starting transfers between devices  56.6 us (23%)
  waiting for transfers between devices  39.2 us (16%)
    unnamed x20, local copies, waits for them, and re-layouts  33.9 us
    ppermute x12, starting transfers between devices, with_halo_2(): lax.ppermute(head, axis, [((i + 1) % count, i) for i in range(count)])  32.2 us
    ppermute x12, waiting for transfers between devices, with_halo_2(): lax.ppermute(tail, axis, [(i, (i + 1) % count) for i in range(count)])  27 us
    mul x1, other arithmetic, body(): ocean * (centre - (flux_east[:, :, 1:] - flux_east[:, :, :-1]) - (flux_no...  20.2 us
    slice x2, local copies, waits for them, and re-layouts, with_halo(): last = lax.slice_in_dim(array, length - width, length, axis=dim)  16.7 us
    mul x1, other arithmetic, body(): analyzed = outer_rim * rim_scale  14.5 us
    unnamed x6, other arithmetic  14.3 us
    scatter x1, local copies, waits for them, and re-layouts, body(): outbox = jnp.zeros((3, devices, slot_cap), jnp.float32).at[:, owners, slo...  11.5 us
  transfers between devices with their start and end apart: 30, of which 12 were waited for; matrix products, arithmetic and copies ran while one was open for 26% of the time, Pallas kernels for 0%

commit v1 on v0

--- a/solution.py
+++ b/solution.py
@@ -77,7 +77,10 @@
         .reshape(3, lat_count, lon_count, slot_cap)
     )
     arrived = lax.all_to_all(
-        lax.all_to_all(outbox, "lat", split_axis=1, concat_axis=1, tiled=True),
+        jnp.concatenate(
+            lax.all_to_all(jnp.stack(jnp.split(outbox, lax.axis_size("lat"), axis=1)), "lat", 0, 0),
+            axis=1,
+        ),
         "lon",
         split_axis=2,
         concat_axis=2,

time: 247 us -> 247 us (level)
    unnamed x20 -> x24, local copies, waits for them, and re-layouts: 33.9 us -> 34.4 us
    unnamed x6 -> x7, other arithmetic: 14.3 us -> 14.3 us
  transfers between devices with their start and end apart: 30 -> 30, of which waited for: 12 -> 12; matrix products, arithmetic and copies ran while one was open for 26% -> 27% of each run, Pallas kernels for 0% -> 0%
where the time goes in v1:
time: 247 us; the launch traced here: 246 us
  local copies, waits for them, and re-layouts  75.6 us (31%)
  other arithmetic  73.8 us (30%)
  starting transfers between devices  56.6 us (23%)
  waiting for transfers between devices  39.2 us (16%)
    unnamed x24, local copies, waits for them, and re-layouts  34.4 us
    ppermute x12, starting transfers between devices, with_halo_2(): lax.ppermute(head, axis, [((i + 1) % count, i) for i in range(count)])  32.2 us
    ppermute x12, waiting for transfers between devices, with_halo_2(): lax.ppermute(tail, axis, [(i, (i + 1) % count) for i in range(count)])  27 us
    mul x1, other arithmetic, body(): ocean * (centre - (flux_east[:, :, 1:] - flux_east[:, :, :-1]) - (flux_no...  20.3 us
    slice x2, local copies, waits for them, and re-layouts, with_halo(): last = lax.slice_in_dim(array, length - width, length, axis=dim)  16.7 us
    mul x1, other arithmetic, body(): analyzed = outer_rim * rim_scale  14.5 us
    unnamed x7, other arithmetic  14.3 us
    scatter x1, local copies, waits for them, and re-layouts, body(): outbox = jnp.zeros((3, devices, slot_cap), jnp.float32).at[:, owners, slo...  11.5 us
  transfers between devices with their start and end apart: 30, of which 12 were waited for; matrix products, arithmetic and copies ran while one was open for 27% of the time, Pallas kernels for 0%

profile of v1, /device:TPU:1, one launch (start us, length us, event | category | flops | bytes accessed | tf_op | source)
XLA Modules:
  0.0 246.5 jit_solution(8220138398501749848)
XLA Ops:
  9.9 11.5 %scatter_fusion = f32[3,128,8]{0,2,1:T(8,128)S(1)} fusion(f32[3,128,8]{0,2,1:T(8,128)S(1)} %broadcast_in_dim.13, s32[256]{0:T(256)S(1)} %bitcast.45, f32[256,3]{1,0:T(8,128)S(1)} %copy.61), kind=kCustom, calls=%fused_computation.1 | custom fusion | bytes 11264 | tf_op jit(solution)/shard_map/scatter | solution.py:76
  22.7 3.3 %all-to-all-start = ((f32[4,1,768]{2,1,0:T(1,128)}), f32[4,1,768]{2,1,0:T(1,128)S(1)}, u32[]{:S(2)}, u32[]{:S(2)}) async-start(f32[4,1,768]{2,1,0:T(1,128)} %reshape.172), calls=%async_computation | async-start | bytes 24576 | tf_op jit(solution)/shard_map/all_to_all | solution.py:81
  25.9 4.8 %reduce_sum.22 = f32[8,256]{1,0:T(8,128)S(1)} reduce(f32[1296,8,256]{2,1,0:T(8,128)} %param.7, f32[]{:T(128)} %constant.15.clone.1), dimensions={0}, to_apply=%region_2.3 | reduce | flops 2652160 | bytes 10625028 | tf_op jit(solution)/shard_map/reduce_sum | solution.py:64
  35.2 7.7 %all-to-all-start.1 = ((f32[3,4,32,8]{3,1,0,2:T(4,128)}), f32[3,4,32,8]{3,1,0,2:T(4,128)S(1)}, u32[]{:S(2)}, u32[]{:S(2)}) async-start(f32[3,4,32,8]{3,1,0,2:T(4,128)} %copy.66), calls=%async_computation.1 | async-start | bytes 393216 | tf_op jit(solution)/shard_map/all_to_all | solution.py:79
  43.0 8.2 %all-to-all-done.1 = f32[3,4,32,8]{3,1,0,2:T(4,128)S(1)} async-done(((f32[3,4,32,8]{3,1,0,2:T(4,128)}), f32[3,4,32,8]{3,1,0,2:T(4,128)S(1)}, u32[]{:S(2)}, u32[]{:S(2)}) %all-to-all-start.1) | async-done | bytes 12320 | tf_op jit(solution)/shard_map/all_to_all | solution.py:79
  51.9 6.2 %gather_fusion = f32[1024]{0:T(1024)S(1)} fusion(f32[2048]{0:T(1024)S(1)} %bitcast.44, s32[1024]{0:T(1024)S(1)} %broadcast_clamp_fusion), kind=kCustom, calls=%fused_computation | custom fusion | bytes 12288 | tf_op jit(solution)/shard_map/gather | solution.py:92
  58.1 7.0 %scatter_custom_fusion.1 = f32[4096]{0:T(1024)S(1)} fusion(s32[1024]{0:T(1024)S(1)} %get-tuple-element.68, f32[1024]{0:T(1024)S(1)} %subtract_multiply_fusion, f32[]{:T(128)} %constant.15.clone.1), kind=kCustom, calls=%fused_computation.183 | custom fusion | flops 1024 | bytes 16388
  65.1 7.1 %scatter_fusion.1 = f32[4096]{0:T(1024)S(1)} fusion(f32[4096]{0:T(1024)S(1)} %scatter_custom_fusion.1, s32[1024]{0:T(1024)S(1)} %get-tuple-element.67, f32[1024]{0:T(1024)S(1)} %reshape.162), kind=kCustom, calls=%fused_computation.3 | custom fusion | flops 1024 | bytes 16384
  83.3 9.2 %fusion.102 = (f32[1296,1,256]{2,1,0:T(1,128)S(1)}, f32[1296,1,256]{2,1,0:T(1,128)S(1)}) fusion(f32[1296,8,256]{2,1,0:T(8,128)} %param.7), kind=kLoop, calls=%fused_computation.206 | loop fusion | bytes 5308416 | tf_op jit(solution)/shard_map/slice | solution.py:16
  93.7 5.8 %collective-permute-start.15 = (f32[2,12,2]{2,1,0:T(8,128)S(1)}, f32[2,12,2]{2,1,0:T(8,128)S(1)}, u32[]{:S(2)}, u32[]{:S(2)}) collective-permute-start(f32[2,12,2]{2,1,0:T(8,128)S(1)} %get-tuple-element.33), channel_id=1, source_target_pairs={{1,0},{2,1},{3,2},{4,3},{5,4},{6,5},{7,6},{8,7},{9,8},{10,9},{11,1... | collective-permute-start | bytes 584 | tf_op jit(solution)/shard_map/ppermute | solution.py:40
  103.9 7.5 %fusion.103 = (f32[1296,8,1]{2,1,0:T(8,128)}, f32[1296,8,1]{2,1,0:T(8,128)}) fusion(f32[1296,8,256]{2,1,0:T(8,128)} %param.7), kind=kLoop, calls=%fused_computation.207 | loop fusion | bytes 165888 | tf_op jit(solution)/shard_map/slice | solution.py:16
  111.4 20.1 %collective-permute-done.16 = f32[2,2,256]{2,1,0:T(2,128)S(1)} collective-permute-done((f32[2,2,256]{2,1,0:T(2,128)S(1)}, f32[2,2,256]{2,1,0:T(2,128)S(1)}, u32[]{:S(2)}, u32[]{:S(2)}) %collective-permute-start.16) | collective-permute-done | bytes 4128 | tf_op jit(solution)/shard_map/ppermute | solution.py:38
  133.3 4.1 %copy.75 = f32[1296,8,1]{0,1,2:T(8,128)S(1)} copy(f32[1296,8,1]{2,1,0:T(8,128)} %get-tuple-element.21) | data formatting | bytes 82944
  140.8 12.4 %copy.56 = f32[1296,8,256]{0,2,1:T(8,128)} copy(f32[1296,8,256]{2,1,0:T(8,128)} %param.7) | data formatting | bytes 21233664 | tf_op args[0]
  153.2 4.1 %copy.72 = f32[1296,8,1]{0,1,2:T(8,128)S(1)} copy(f32[1296,8,1]{2,1,0:T(8,128)} %get-tuple-element.20) | data formatting | bytes 82944
  157.4 5.2 %collective-permute-start.23 = (f32[2,12,2]{2,1,0:T(8,128)S(1)}, f32[2,12,2]{2,1,0:T(8,128)S(1)}, u32[]{:S(2)}, u32[]{:S(2)}) collective-permute-start(f32[2,12,2]{2,1,0:T(8,128)S(1)} %get-tuple-element.29), channel_id=1, source_target_pairs={{1,0},{2,1},{3,2},{4,3},{5,4},{6,5},{7,6},{8,7},{9,8},{10,9},{11,1... | collective-permute-start | bytes 584 | tf_op jit(solution)/shard_map/ppermute | solution.py:40
  168.7 2.8 %collective-permute-start = (f32[1296,8,1]{0,1,2:T(8,128)S(1)}, f32[1296,8,1]{0,1,2:T(8,128)S(1)}, u32[]{:S(2)}, u32[]{:S(2)}) collective-permute-start(f32[1296,8,1]{0,1,2:T(8,128)S(1)} %copy.72), channel_id=1, source_target_pairs={{0,1},{1,2},{2,3},{3,4},{4,5},{5,6},{6,7},{7,8},{8,9},{9,10},{10,1... | collective-permute-start | bytes 124424 | tf_op jit(solution)/shard_map/ppermute | solution.py:19
  171.6 4.1 %collective-permute-done.26 = f32[10,1]{1,0:T(8,128)S(1)} collective-permute-done((f32[10,1]{1,0:T(8,128)S(1)}, f32[10,1]{1,0:T(8,128)S(1)}, u32[]{:S(2)}, u32[]{:S(2)}) %collective-permute-start.26) | collective-permute-done | bytes 72 | tf_op jit(solution)/shard_map/ppermute | solution.py:38
  175.7 6.1 %collective-permute-start.27 = (f32[10,1]{1,0:T(8,128)S(1)}, f32[10,1]{1,0:T(8,128)S(1)}, u32[]{:S(2)}, u32[]{:S(2)}) collective-permute-start(f32[10,1]{1,0:T(8,128)S(1)} %get-tuple-element.52), channel_id=1, source_target_pairs={{1,0},{2,1},{3,2},{4,3},{5,4},{6,5},{7,6},{8,7},{9,8},{10,9},{11,1... | collective-permute-start | bytes 128 | tf_op jit(solution)/shard_map/ppermute | solution.py:40
  186.4 14.5 %fusion = f32[1296,10,258]{0,2,1:T(8,128)S(1)} fusion(f32[1296,8,1]{0,2,1:T(1,128)S(1)} %copy.82, f32[1296,8,1]{0,2,1:T(1,128)S(1)} %copy.81, f32[1296,1,256]{0,2,1:T(8,128)S(1)} %copy.57, f32[1296,8,256]{0,2,1:T(8,128)} %copy.56, f32[1296,1,256]{0,2,1:T(8,128)S(1)} %copy.55, f32[10,258]{1,0:T(8,128)S(1)} %pad_maximum_fusion.33), kind=kLoop, calls=%fused_computation.5 | loop fusion | flops 30093120 | bytes 26739024 | tf_op jit(solution)/shard_map/mul | solution.py:116
  200.9 5.9 %fusion.6 = f32[1296,8,257]{0,2,1:T(8,128)} fusion(f32[1296,10,258]{0,2,1:T(8,128)S(1)} %fusion, f32[8,257]{1,0:T(8,128)S(1)} %get-tuple-element.38, f32[8,257]{1,0:T(8,128)S(1)} %get-tuple-element.37, f32[1296]{0:T(1024)S(1)} %get-tuple-element.9, f32[1296]{0:T(1024)S(1)} %get-tuple-element.8), kind=kLoop, calls=%fused_computation.17 | loop fusion | flops 13322880 | bytes 32001728 | tf_op jit(solution)/shard_map/mul | solution.py:122
  206.8 7.3 %fusion.3 = f32[1296,9,256]{0,2,1:T(8,128)} fusion(f32[1296,10,258]{0,2,1:T(8,128)S(1)} %fusion, f32[9,256]{1,0:T(8,128)S(1)} %get-tuple-element.40, f32[9,256]{1,0:T(8,128)S(1)} %get-tuple-element.39, f32[1296]{0:T(1024)S(1)} %get-tuple-element.10, f32[1296]{0:T(1024)S(1)} %get-tuple-element.11), kind=kLoop, calls=%fused_computation.12 | loop fusion | flops 14929920 | bytes 35860608 | tf_op jit(solution)/shard_map/mul | solution.py:132
  214.1 20.3 %fusion.8 = f32[1296,8,256]{0,2,1:T(8,128)} fusion(f32[1296,9,256]{0,2,1:T(8,128)} %fusion.3, f32[1296,8,257]{0,2,1:T(8,128)} %fusion.6, f32[1296,10,258]{0,2,1:T(8,128)S(1)} %fusion, f32[8,256]{1,0:T(8,128)S(1)} %convert_element_type.28), kind=kLoop, calls=%fused_computation.21 | loop fusion | flops 13271040 | bytes 63709184 | tf_op jit(solution)/shard_map/mul | solution.py:140
  234.4 12.1 %copy.71 = f32[1296,8,256]{2,1,0:T(8,128)} copy(f32[1296,8,256]{0,2,1:T(8,128)} %fusion.8) | data formatting | bytes 21233664
  (143 shorter events, 48.1 us)
Async XLA Ops:
  1.5 29.3 %collective-permute-start.8 = (s32[2,256]{1,0:T(2,128)S(1)}, s32[2,256]{1,0:T(2,128)S(1)}, u32[]{:S(2)}, u32[]{:S(2)}) collective-permute-start(s32[2,256]{1,0:T(2,128)S(1)} %get-tuple-element.65), channel_id=1, source_target_pairs={{0,32},{32,64},{64,96},{96,0},{1,33},{33,65},{65,97},{97,1},{2,34}... | collective-permute-start | bytes 6152 | tf_op jit(solution)/shard_map/ppermute | solution.py:38
  3.9 26.9 %collective-permute-start.9 = (s32[2,256]{1,0:T(2,128)S(1)}, s32[2,256]{1,0:T(2,128)S(1)}, u32[]{:S(2)}, u32[]{:S(2)}) collective-permute-start(s32[2,256]{1,0:T(2,128)S(1)} %get-tuple-element.66), channel_id=1, source_target_pairs={{32,0},{64,32},{96,64},{0,96},{33,1},{65,33},{97,65},{1,97},{34,2}... | collective-permute-start | bytes 6152 | tf_op jit(solution)/shard_map/ppermute | solution.py:40
  22.7 10.4 %all-to-all-start = ((f32[4,1,768]{2,1,0:T(1,128)}), f32[4,1,768]{2,1,0:T(1,128)S(1)}, u32[]{:S(2)}, u32[]{:S(2)}) async-start(f32[4,1,768]{2,1,0:T(1,128)} %reshape.172), calls=%async_computation | async-start | bytes 24576 | tf_op jit(solution)/shard_map/all_to_all | solution.py:81
  30.9 11.9 %collective-permute-start.10 = (s32[12,2]{1,0:T(8,128)S(1)}, s32[12,2]{1,0:T(8,128)S(1)}, u32[]{:S(2)}, u32[]{:S(2)}) collective-permute-start(s32[12,2]{1,0:T(8,128)S(1)} %get-tuple-element.59), channel_id=1, source_target_pairs={{0,1},{1,2},{2,3},{3,4},{4,5},{5,6},{6,7},{7,8},{8,9},{9,10},{10,1... | collective-permute-start | bytes 296 | tf_op jit(solution)/shard_map/ppermute | solution.py:38
  33.1 9.8 %collective-permute-start.11 = (s32[12,2]{1,0:T(8,128)S(1)}, s32[12,2]{1,0:T(8,128)S(1)}, u32[]{:S(2)}, u32[]{:S(2)}) collective-permute-start(s32[12,2]{1,0:T(8,128)S(1)} %get-tuple-element.60), channel_id=1, source_target_pairs={{1,0},{2,1},{3,2},{4,3},{5,4},{6,5},{7,6},{8,7},{9,8},{10,9},{11,1... | collective-permute-start | bytes 296 | tf_op jit(solution)/shard_map/ppermute | solution.py:40
  35.2 16.0 %all-to-all-start.1 = ((f32[3,4,32,8]{3,1,0,2:T(4,128)}), f32[3,4,32,8]{3,1,0,2:T(4,128)S(1)}, u32[]{:S(2)}, u32[]{:S(2)}) async-start(f32[3,4,32,8]{3,1,0,2:T(4,128)} %copy.66), calls=%async_computation.1 | async-start | bytes 393216 | tf_op jit(solution)/shard_map/all_to_all | solution.py:79
  80.6 13.1 %collective-permute-start.12 = (f32[2,2,256]{2,1,0:T(2,128)S(1)}, f32[2,2,256]{2,1,0:T(2,128)S(1)}, u32[]{:S(2)}, u32[]{:S(2)}) collective-permute-start(f32[2,2,256]{2,1,0:T(2,128)S(1)} %get-tuple-element.57), channel_id=1, source_target_pairs={{0,32},{32,64},{64,96},{96,0},{1,33},{33,65},{65,97},{97,1},{2,34}... | collective-permute-start | bytes 12296 | tf_op jit(solution)/shard_map/ppermute | solution.py:38
  81.4 12.2 %collective-permute-start.13 = (f32[2,2,256]{2,1,0:T(2,128)S(1)}, f32[2,2,256]{2,1,0:T(2,128)S(1)}, u32[]{:S(2)}, u32[]{:S(2)}) collective-permute-start(f32[2,2,256]{2,1,0:T(2,128)S(1)} %get-tuple-element.58), channel_id=1, source_target_pairs={{32,0},{64,32},{96,64},{0,96},{33,1},{65,33},{97,65},{1,97},{34,2}... | collective-permute-start | bytes 12296 | tf_op jit(solution)/shard_map/ppermute | solution.py:40
  92.6 90.2 %collective-permute-start.2 = (f32[1296,1,256]{2,0,1:T(8,128)S(1)}, f32[1296,1,256]{2,0,1:T(8,128)}, u32[]{:S(2)}, u32[]{:S(2)}) collective-permute-start(f32[1296,1,256]{2,0,1:T(8,128)S(1)} %copy.74), channel_id=1, source_target_pairs={{32,0},{64,32},{96,64},{0,96},{33,1},{65,33},{97,65},{1,97},{34,2}... | collective-permute-start | bytes 3981320 | tf_op jit(solution)/shard_map/ppermute | solution.py:20
  93.7 6.7 %collective-permute-start.15 = (f32[2,12,2]{2,1,0:T(8,128)S(1)}, f32[2,12,2]{2,1,0:T(8,128)S(1)}, u32[]{:S(2)}, u32[]{:S(2)}) collective-permute-start(f32[2,12,2]{2,1,0:T(8,128)S(1)} %get-tuple-element.33), channel_id=1, source_target_pairs={{1,0},{2,1},{3,2},{4,3},{5,4},{6,5},{7,6},{8,7},{9,8},{10,9},{11,1... | collective-permute-start | bytes 584 | tf_op jit(solution)/shard_map/ppermute | solution.py:40
  99.7 85.0 %collective-permute-start.1 = (f32[1296,1,256]{2,0,1:T(8,128)S(1)}, f32[1296,1,256]{2,0,1:T(8,128)}, u32[]{:S(2)}, u32[]{:S(2)}) collective-permute-start(f32[1296,1,256]{2,0,1:T(8,128)S(1)} %copy.73), channel_id=1, source_target_pairs={{0,32},{32,64},{64,96},{96,0},{1,33},{33,65},{65,97},{97,1},{2,34}... | collective-permute-start | bytes 3981320 | tf_op jit(solution)/shard_map/ppermute | solution.py:19
  101.1 30.4 %collective-permute-start.16 = (f32[2,2,256]{2,1,0:T(2,128)S(1)}, f32[2,2,256]{2,1,0:T(2,128)S(1)}, u32[]{:S(2)}, u32[]{:S(2)}) collective-permute-start(f32[2,2,256]{2,1,0:T(2,128)S(1)} %get-tuple-element.55), channel_id=1, source_target_pairs={{0,32},{32,64},{64,96},{96,0},{1,33},{33,65},{65,97},{97,1},{2,34}... | collective-permute-start | bytes 12296 | tf_op jit(solution)/shard_map/ppermute | solution.py:38
  101.6 29.9 %collective-permute-start.17 = (f32[2,2,256]{2,1,0:T(2,128)S(1)}, f32[2,2,256]{2,1,0:T(2,128)S(1)}, u32[]{:S(2)}, u32[]{:S(2)}) collective-permute-start(f32[2,2,256]{2,1,0:T(2,128)S(1)} %get-tuple-element.56), channel_id=1, source_target_pairs={{32,0},{64,32},{96,64},{0,96},{33,1},{65,33},{97,65},{1,97},{34,2}... | collective-permute-start | bytes 12296 | tf_op jit(solution)/shard_map/ppermute | solution.py:40
  131.6 6.0 %collective-permute-start.19 = (f32[2,12,2]{2,1,0:T(8,128)S(1)}, f32[2,12,2]{2,1,0:T(8,128)S(1)}, u32[]{:S(2)}, u32[]{:S(2)}) collective-permute-start(f32[2,12,2]{2,1,0:T(8,128)S(1)} %get-tuple-element.31), channel_id=1, source_target_pairs={{1,0},{2,1},{3,2},{4,3},{5,4},{6,5},{7,6},{8,7},{9,8},{10,9},{11,1... | collective-permute-start | bytes 584 | tf_op jit(solution)/shard_map/ppermute | solution.py:40
  132.9 4.7 %collective-permute-start.18 = (f32[2,12,2]{2,1,0:T(8,128)S(1)}, f32[2,12,2]{2,1,0:T(8,128)S(1)}, u32[]{:S(2)}, u32[]{:S(2)}) collective-permute-start(f32[2,12,2]{2,1,0:T(8,128)S(1)} %get-tuple-element.32), channel_id=1, source_target_pairs={{0,1},{1,2},{2,3},{3,4},{4,5},{5,6},{6,7},{7,8},{8,9},{9,10},{10,1... | collective-permute-start | bytes 584 | tf_op jit(solution)/shard_map/ppermute | solution.py:38
  137.4 45.3 %collective-permute-start.3 = (f32[1296,8,1]{0,1,2:T(8,128)S(1)}, f32[1296,8,1]{0,1,2:T(8,128)S(1)}, u32[]{:S(2)}, u32[]{:S(2)}) collective-permute-start(f32[1296,8,1]{0,1,2:T(8,128)S(1)} %copy.75), channel_id=1, source_target_pairs={{1,0},{2,1},{3,2},{4,3},{5,4},{6,5},{7,6},{8,7},{9,8},{10,9},{11,1... | collective-permute-start | bytes 124424 | tf_op jit(solution)/shard_map/ppermute | solution.py:20
  138.0 19.3 %collective-permute-start.20 = (f32[2,2,256]{2,1,0:T(2,128)S(1)}, f32[2,2,256]{2,1,0:T(2,128)S(1)}, u32[]{:S(2)}, u32[]{:S(2)}) collective-permute-start(f32[2,2,256]{2,1,0:T(2,128)S(1)} %get-tuple-element.53), channel_id=1, source_target_pairs={{0,32},{32,64},{64,96},{96,0},{1,33},{33,65},{65,97},{97,1},{2,34}... | collective-permute-start | bytes 12296 | tf_op jit(solution)/shard_map/ppermute | solution.py:38
  138.0 19.2 %collective-permute-start.21 = (f32[2,2,256]{2,1,0:T(2,128)S(1)}, f32[2,2,256]{2,1,0:T(2,128)S(1)}, u32[]{:S(2)}, u32[]{:S(2)}) collective-permute-start(f32[2,2,256]{2,1,0:T(2,128)S(1)} %get-tuple-element.54), channel_id=1, source_target_pairs={{32,0},{64,32},{96,64},{0,96},{33,1},{65,33},{97,65},{1,97},{34,2}... | collective-permute-start | bytes 12296 | tf_op jit(solution)/shard_map/ppermute | solution.py:40
  157.4 6.0 %collective-permute-start.23 = (f32[2,12,2]{2,1,0:T(8,128)S(1)}, f32[2,12,2]{2,1,0:T(8,128)S(1)}, u32[]{:S(2)}, u32[]{:S(2)}) collective-permute-start(f32[2,12,2]{2,1,0:T(8,128)S(1)} %get-tuple-element.29), channel_id=1, source_target_pairs={{1,0},{2,1},{3,2},{4,3},{5,4},{6,5},{7,6},{8,7},{9,8},{10,9},{11,1... | collective-permute-start | bytes 584 | tf_op jit(solution)/shard_map/ppermute | solution.py:40
  164.7 3.9 %collective-permute-start.24 = (f32[1,256]{1,0:T(1,128)S(1)}, f32[1,256]{1,0:T(1,128)S(1)}, u32[]{:S(2)}, u32[]{:S(2)}) collective-permute-start(f32[1,256]{1,0:T(1,128)S(1)} %get-tuple-element.63), channel_id=1, source_target_pairs={{0,32},{32,64},{64,96},{96,0},{1,33},{33,65},{65,97},{97,1},{2,34}... | collective-permute-start | bytes 3080 | tf_op jit(solution)/shard_map/ppermute | solution.py:38
  164.8 6.8 %collective-permute-start.25 = (f32[1,256]{1,0:T(1,128)S(1)}, f32[1,256]{1,0:T(1,128)S(1)}, u32[]{:S(2)}, u32[]{:S(2)}) collective-permute-start(f32[1,256]{1,0:T(1,128)S(1)} %get-tuple-element.64), channel_id=1, source_target_pairs={{32,0},{64,32},{96,64},{0,96},{33,1},{65,33},{97,65},{1,97},{34,2}... | collective-permute-start | bytes 3080 | tf_op jit(solution)/shard_map/ppermute | solution.py:40
  168.7 14.1 %collective-permute-start = (f32[1296,8,1]{0,1,2:T(8,128)S(1)}, f32[1296,8,1]{0,1,2:T(8,128)S(1)}, u32[]{:S(2)}, u32[]{:S(2)}) collective-permute-start(f32[1296,8,1]{0,1,2:T(8,128)S(1)} %copy.72), channel_id=1, source_target_pairs={{0,1},{1,2},{2,3},{3,4},{4,5},{5,6},{6,7},{7,8},{8,9},{9,10},{10,1... | collective-permute-start | bytes 124424 | tf_op jit(solution)/shard_map/ppermute | solution.py:19
  171.6 4.1 %collective-permute-start.26 = (f32[10,1]{1,0:T(8,128)S(1)}, f32[10,1]{1,0:T(8,128)S(1)}, u32[]{:S(2)}, u32[]{:S(2)}) collective-permute-start(f32[10,1]{1,0:T(8,128)S(1)} %get-tuple-element.51), channel_id=1, source_target_pairs={{0,1},{1,2},{2,3},{3,4},{4,5},{5,6},{6,7},{7,8},{8,9},{9,10},{10,1... | collective-permute-start | bytes 128 | tf_op jit(solution)/shard_map/ppermute | solution.py:38
  175.7 6.9 %collective-permute-start.27 = (f32[10,1]{1,0:T(8,128)S(1)}, f32[10,1]{1,0:T(8,128)S(1)}, u32[]{:S(2)}, u32[]{:S(2)}) collective-permute-start(f32[10,1]{1,0:T(8,128)S(1)} %get-tuple-element.52), channel_id=1, source_target_pairs={{1,0},{2,1},{3,2},{4,3},{5,4},{6,5},{7,6},{8,7},{9,8},{10,9},{11,1... | collective-permute-start | bytes 128 | tf_op jit(solution)/shard_map/ppermute | solution.py:40
  (10 other events, 184.9 us)
